TPU v7x, 128 devices: a whole 4x4x4 slice. The times are simulated.
128 devices in a mesh: dp: 8 (over x, core), seq: 16 (over z, y).
Axes of the slice: x: 4, y: 4, z: 4, core: 2. Of those that a mesh axis runs over, the one named last changes fastest.
Arguments:
- text_rows: bfloat16 [16384, 8192], P(('dp', 'seq')), may hold values from -6 to 6
- image_rows: bfloat16 [32, 256, 8192], P('dp', 'seq'), may hold values from -6 to 6
- tile_group: int32 [32], replicated, may hold values from 0 to 7, as said below
- tile_offset: int32 [32], replicated, may hold values from 0 to 1792, as said below
- seq_len: int32 [8], P('dp'), may hold values from 1024 to 2048, as said below
- doc_ids: int32 [8, 2048], P('dp'), may hold values from 0 to 7, never falling along the last dimension, each value on 1 to 512 neighbouring positions
- norm_gain: float32 [8192], replicated, may hold values from 0.1 to 1.9
- q_weight: bfloat16 [8192, 8192], P(None, 'seq'), may hold values from -0.0625 to 0.0625
- k_weight: bfloat16 [8192, 1024], P(None, 'seq'), may hold values from -0.0625 to 0.0625
- v_weight: bfloat16 [8192, 1024], P(None, 'seq'), may hold values from -0.0625 to 0.0625
- q_bias: float32 [8192], P('seq'), may hold values from -3 to 3
- k_bias: float32 [1024], P('seq'), may hold values from -40 to 40
- v_bias: float32 [1024], P('seq'), may hold values from -3 to 3
Outputs:
- attention: bfloat16 [16384, 8192], P('dp', 'seq')
Inputs may be any that keep to these rules, and one draw needn't show every extreme that they name: `tile_group`: the 4 tiles r * 4 to r * 4 + 3 of each r < 8 go to distinct packed sequences; one packed sequence takes exactly 7 tiles and none takes more. `tile_offset`: the tiles of one packed sequence lie back to back in increasing tile order and end at or before its seq_len. `seq_len`: some packed sequence uses all 2048 positions. `doc_ids`: document ids never fall along a sequence and no document is longer than 512 positions.
All inputs are finite; a program needn't handle non-finite values.
Results may differ from a plain program's by a relative error of at most 0.003.
The roundings to bfloat16 on the way count: a program that leaves them out, or rounds other values in their place, can miss the bound.
Values may be sent and summed in bfloat16 or wider, within the bound.
No kernel may reach another device: no remote copies, remote signals or barrier semaphores. Data moves between devices by JAX's collectives and lax.ppermute only.
A program may use at most 128 MiB of HBM per device.

v0:
```python
import jax
import jax.numpy as jnp
from jax import lax
from jax.sharding import PartitionSpec as P

TR = 256
THETA = 1000000.0
NEGATIVE = -1e30
EPSILON = 1e-06


def swapped(block, axis, bit):
    count = lax.axis_size(axis)
    route = []
    for low in range(count):
        high = low | 1 << bit
        if high != low and high < count:
            route += [(low, high), (high, low)]
    return lax.ppermute(block, axis, route)


def rms_norm(row_block, norm_gain):
    float_rows = row_block.astype(jnp.float32)
    inv_rms = lax.rsqrt(jnp.mean(float_rows * float_rows, axis=-1, keepdims=True) + EPSILON)
    return (float_rows * inv_rms * norm_gain).astype(jnp.bfloat16)


def doc_positions(doc_row):
    indices = jnp.arange(doc_row.shape[0], dtype=jnp.int32)
    starts = jnp.concatenate([jnp.ones((1,), jnp.bool_), doc_row[1:] != doc_row[:-1]])
    first_index = lax.cummax(jnp.where(starts, indices, 0), axis=0)
    return indices - first_index


def rotary(values, position):
    head_dim = values.shape[-1]
    half_dim = head_dim // 2
    frequency = THETA ** (-(jnp.arange(half_dim, dtype=jnp.float32) * 2.0) / head_dim)
    angles = position.astype(jnp.float32)[:, None] * frequency[None, :]
    cosine = jnp.concatenate([jnp.cos(angles), jnp.cos(angles)], axis=-1)
    sine_part = jnp.concatenate([jnp.sin(angles), jnp.sin(angles)], axis=-1)
    if values.ndim == 3:
        cosine = cosine[:, None, :]
        sine_part = sine_part[:, None, :]
    rotated = jnp.concatenate([-values[..., half_dim:], values[..., :half_dim]], axis=-1)
    return values * cosine + rotated * sine_part


def attend(queries, key_rows, value_rows, doc_row, valid_len):
    length, head_count, head_dim = queries.shape
    window = length // 4
    block_rows = min(512, length)
    scale_factor = head_dim ** (-0.5)
    keys_pad = jnp.concatenate([jnp.zeros((window, head_dim), key_rows.dtype), key_rows], axis=0)
    values_pad = jnp.concatenate(
        [jnp.zeros((window, head_dim), value_rows.dtype), value_rows], axis=0
    )
    doc_pad = jnp.concatenate([jnp.full((window,), -1, jnp.int32), doc_row])
    index_pad = jnp.arange(length + window, dtype=jnp.int32) - window

    def one_block(block_step, output):
        row_start = block_step * block_rows
        query_part = lax.dynamic_slice_in_dim(queries, row_start, block_rows, 0)
        key_part = lax.dynamic_slice_in_dim(keys_pad, row_start, block_rows + window, 0)
        value_part = lax.dynamic_slice_in_dim(values_pad, row_start, block_rows + window, 0)
        doc_part = lax.dynamic_slice_in_dim(doc_pad, row_start, block_rows + window, 0)
        key_index = lax.dynamic_slice_in_dim(index_pad, row_start, block_rows + window, 0)
        query_doc = lax.dynamic_slice_in_dim(doc_row, row_start, block_rows, 0)
        query_index = row_start + jnp.arange(block_rows, dtype=jnp.int32)
        scores = (
            jnp.einsum("qhd,kd->hqk", query_part, key_part, preferred_element_type=jnp.float32)
            * scale_factor
        )
        allowed = (
            (query_doc[:, None] == doc_part[None, :])
            & (key_index[None, :] <= query_index[:, None])
            & (key_index[None, :] < valid_len)
        )
        scores = jnp.where(allowed[None], scores, NEGATIVE)
        row_peak = jnp.max(scores, axis=-1, keepdims=True)
        exponent = jnp.exp(scores - row_peak)
        weights = (exponent / jnp.sum(exponent, axis=-1, keepdims=True)).astype(jnp.bfloat16)
        mixed = jnp.einsum("hqk,kd->qhd", weights, value_part, preferred_element_type=jnp.float32)
        mixed = jnp.where((query_index < valid_len)[:, None, None], mixed, 0.0).astype(jnp.bfloat16)
        return lax.dynamic_update_slice_in_dim(
            output, mixed.reshape(block_rows, head_count * head_dim), row_start, 0
        )

    initial = jnp.zeros((length, head_count * head_dim), jnp.bfloat16)
    return lax.fori_loop(0, length // block_rows, one_block, initial)


def per_device(
    text_rows,
    image_rows,
    tile_group,
    tile_offset,
    seq_len,
    doc_ids,
    norm_gain,
    q_weight,
    k_weight,
    v_weight,
    q_bias,
    k_bias,
    v_bias,
):
    group_count = lax.axis_size("dp")
    member_count = lax.axis_size("seq")
    my_group = lax.axis_index("dp")
    my_member = lax.axis_index("seq")
    tiles_row, piece_rows, feature_count = image_rows.shape
    owned_rows = text_rows.shape[0]
    length = owned_rows * member_count
    window_tiles = max(1, owned_rows // TR)
    capacity = piece_rows * window_tiles
    row_groups = lax.dynamic_slice_in_dim(tile_group, my_group * tiles_row, tiles_row)
    chooser = (row_groups[None, :] == jnp.arange(group_count, dtype=jnp.int32)[:, None]).astype(
        jnp.bfloat16
    )
    outgoing = jnp.einsum(
        "gj,jrd->grd", chooser, image_rows, preferred_element_type=jnp.float32
    ).astype(jnp.bfloat16)
    arrived = lax.all_to_all(outgoing, "dp", split_axis=0, concat_axis=0, tiled=True)
    table_group = tile_group.reshape(group_count, tiles_row)
    table_offset = tile_offset.reshape(group_count, tiles_row)
    matches = table_group == my_group
    present = jnp.any(matches, axis=1)
    offset_from = jnp.sum(jnp.where(matches, table_offset, 0), axis=1)
    within = jnp.arange(piece_rows, dtype=jnp.int32)
    landing = offset_from[:, None] + my_member * piece_rows + within[None, :]
    slot_index = offset_from[:, None] // TR % window_tiles * piece_rows + within[None, :]
    target = jnp.where(present[:, None], landing // owned_rows * capacity + slot_index, -1).reshape(
        -1
    )
    spread = (
        jnp.arange(member_count * capacity, dtype=jnp.int32)[:, None] == target[None, :]
    ).astype(jnp.bfloat16)
    forward = jnp.dot(
        spread,
        arrived.reshape(group_count * piece_rows, feature_count),
        preferred_element_type=jnp.float32,
    ).astype(jnp.bfloat16)
    landed = lax.all_to_all(
        forward.reshape(member_count, capacity, feature_count),
        "seq",
        split_axis=0,
        concat_axis=0,
        tiled=True,
    )
    positions = my_member * owned_rows + jnp.arange(owned_rows, dtype=jnp.int32)
    inside = (
        (tile_group[None, :] == my_group)
        & (tile_offset[None, :] <= positions[:, None])
        & (positions[:, None] < tile_offset[None, :] + TR)
    )
    covered = jnp.any(inside, axis=1)
    tile_start = jnp.sum(jnp.where(inside, tile_offset[None, :], 0), axis=1)
    offset_in = positions - tile_start
    source = (
        offset_in // piece_rows * capacity
        + tile_start // TR % window_tiles * piece_rows
        + offset_in % piece_rows
    )
    source = jnp.where(covered, source, 0)
    image_part = jnp.take(landed.reshape(member_count * capacity, feature_count), source, axis=0)
    merged = jnp.where(covered[:, None], image_part, text_rows)
    normed = rms_norm(merged, norm_gain)
    row_block = lax.all_gather(normed, "seq", axis=0, tiled=True)
    projected = jnp.concatenate(
        [
            jnp.dot(row_block, q_weight, preferred_element_type=jnp.float32),
            jnp.dot(row_block, k_weight, preferred_element_type=jnp.float32),
            jnp.dot(row_block, v_weight, preferred_element_type=jnp.float32),
        ],
        axis=1,
    )
    query_cols = q_weight.shape[1]
    half_cols = k_weight.shape[1]
    head_dim = 2 * half_cols
    query_raw = projected[:, :query_cols] + q_bias
    own_half = projected[:, query_cols:] + jnp.concatenate([k_bias, v_bias])
    other_half = swapped(own_half, "seq", 0)
    is_lower = my_member % 2 == 0
    lower_half = jnp.where(is_lower, own_half, other_half)
    upper_half = jnp.where(is_lower, other_half, own_half)
    key_raw = jnp.concatenate([lower_half[:, :half_cols], upper_half[:, :half_cols]], axis=1)
    value_rows = jnp.concatenate(
        [lower_half[:, half_cols:], upper_half[:, half_cols:]], axis=1
    ).astype(jnp.bfloat16)
    doc_row = doc_ids[0]
    in_doc = doc_positions(doc_row)
    queries = rotary(query_raw.reshape(length, query_cols // head_dim, head_dim), in_doc).astype(
        jnp.bfloat16
    )
    key_rows = rotary(key_raw, in_doc).astype(jnp.bfloat16)
    return attend(queries, key_rows, value_rows, doc_row, seq_len[0])


def solution(mesh):
    return jax.shard_map(
        per_device,
        mesh=mesh,
        in_specs=(
            P(("dp", "seq"), None),
            P("dp", "seq", None),
            P(),
            P(),
            P("dp"),
            P("dp", None),
            P(),
            P(None, "seq"),
            P(None, "seq"),
            P(None, "seq"),
            P("seq"),
            P("seq"),
            P("seq"),
        ),
        out_specs=P("dp", "seq"),
        check_vma=False,
    )
```

profile of v0, /device:TPU:1, one launch (start us, length us, event | category | flops | bytes accessed | tf_op | source)
XLA Modules:
  0.0 477.6 jit_solution(18265404585857604997)
XLA Ops:
  6.5 0.8 dynamic_slice.45
  7.4 0.4 copy-done
  7.8 1.5 convolution_convert_fusion.1
  9.3 2.5 copy.45
  11.7 5.8 %all-to-all-start = ((bf16[8,16,8192]{2,1,0:T(8,128)(2,1)}), bf16[8,16,8192]{2,1,0:T(8,128)(2,1)S(1)}, u32[]{:S(2)}, u32[]{:S(2)}) async-start(bf16[8,16,8192]{2,1,0:T(8,128)(2,1)} %copy.45), calls=%async_computation | async-start | bytes 4194304 | tf_op jit(solution)/shard_map/all_to_all | solution.py:124
  18.4 25.3 %all-to-all-done = bf16[8,16,8192]{2,1,0:T(8,128)(2,1)S(1)} async-done(((bf16[8,16,8192]{2,1,0:T(8,128)(2,1)}), bf16[8,16,8192]{2,1,0:T(8,128)(2,1)S(1)}, u32[]{:S(2)}, u32[]{:S(2)}) %all-to-all-start) | async-done | bytes 2097184 | tf_op jit(solution)/shard_map/all_to_all | solution.py:124
  43.7 3.2 convolution_convert_fusion
  47.0 7.8 %all-to-all-start.1 = ((bf16[16,16,8192]{2,1,0:T(8,128)(2,1)}), bf16[16,16,8192]{2,1,0:T(8,128)(2,1)}, u32[]{:S(2)}, u32[]{:S(2)}) async-start(bf16[16,16,8192]{2,1,0:T(8,128)(2,1)} %bitcast.73), calls=%async_computation.1 | async-start | bytes 8388608 | tf_op jit(solution)/shard_map/all_to_all | solution.py:144
  55.1 61.4 %all-to-all-done.1 = bf16[16,16,8192]{2,1,0:T(8,128)(2,1)} async-done(((bf16[16,16,8192]{2,1,0:T(8,128)(2,1)}), bf16[16,16,8192]{2,1,0:T(8,128)(2,1)}, u32[]{:S(2)}, u32[]{:S(2)}) %all-to-all-start.1) | async-done | bytes 4194336 | tf_op jit(solution)/shard_map/all_to_all | solution.py:144
  116.6 6.5 %gather_fusion = bf16[128,8192]{1,0:T(8,128)(2,1)S(1)} fusion(bf16[256,8192]{1,0:T(8,128)(2,1)} %bitcast.9, s32[1024]{0:T(1024)S(1)} %pad_clamp_fusion), kind=kCustom, calls=%fused_computation | custom fusion | bytes 4194816 | tf_op jit(solution)/shard_map/jit(_take)/gather | solution.py:166
  123.1 2.8 fusion.34
  125.9 1.9 fusion.36
  128.8 3.0 multiply_cosine_fusion
  131.7 192.0 %all-gather.2.cloned.1.call-done = bf16[2048,8192]{1,0:T(8,128)(2,1)} async-done(((bf16[128,8192]{1,0:T(8,128)(2,1)}), bf16[2048,8192]{1,0:T(8,128)(2,1)}) %all-gather.2.cloned.1.call-update) | async-done | bytes 33554448 | tf_op jit(solution)/shard_map/all_gather | solution.py:169
  323.7 16.2 %fusion.65 = f32[2048,64]{0,1:T(8,128)S(1)} fusion(bf16[2048,8192]{1,0:T(8,128)(2,1)} %all-gather.2.cloned.1.call-done, bf16[8192,64]{0,1:T(8,128)(2,1)S(1)} %copy-done.5), kind=kOutput, calls=%fused_computation.114 | convolution fusion | flops 2147483648 | bytes 35127296 | tf_op jit(solution)/shard_map/dot_general | solution.py:174
  339.9 16.2 %fusion.64 = f32[2048,64]{0,1:T(8,128)S(1)} fusion(bf16[2048,8192]{1,0:T(8,128)(2,1)} %all-gather.2.cloned.1.call-done, bf16[8192,64]{0,1:T(8,128)(2,1)S(1)} %copy-done.6), kind=kOutput, calls=%fused_computation.113 | convolution fusion | flops 2147483648 | bytes 35127296 | tf_op jit(solution)/shard_map/dot_general | solution.py:173
  356.2 1.3 collective-permute-start
  357.5 25.0 %convolution_add_fusion = f32[2048,512]{0,1:T(8,128)} fusion(bf16[2048,8192]{1,0:T(8,128)(2,1)} %all-gather.2.cloned.1.call-done, bf16[8192,512]{1,0:T(8,128)(2,1)} %param.22, f32[512]{0:T(512)S(1)} %copy-done.10), kind=kOutput, calls=%fused_computation.43 | convolution fusion | flops 17180917760 | bytes 46139392 | tf_op jit(solution)/shard_map/dot_general | solution.py:172
  382.5 5.3 %copy.47 = f32[2048,4,128]{2,0,1:T(8,128)} copy(f32[2048,4,128]{0,2,1:T(8,128)} %bitcast.76) | data formatting | bytes 8388608 | tf_op jit(solution)/shard_map/reshape | solution.py:193
  387.8 7.9 %slice_negate_fusion = (f32[2048,4,64]{2,0,1:T(8,128)}, f32[2048,4,64]{2,0,1:T(8,128)}) fusion(f32[2048,4,128]{2,0,1:T(8,128)} %copy.47), kind=kLoop, calls=%fused_computation.39 | loop fusion | flops 524288 | bytes 8388608 | tf_op jit(solution)/shard_map/neg | solution.py:45
  396.0 0.8 slice.62
  397.0 1.1 pad_maximum_fusion
  398.7 1.9 fusion.44
  400.6 2.0 concatenate.52
  402.5 7.1 %fusion.38 = bf16[2048,4,128]{2,0,1:T(8,128)(2,1)} fusion(f32[2048,4,64]{2,0,1:T(8,128)} %get-tuple-element.221, f32[2048,4,64]{2,0,1:T(8,128)} %get-tuple-element.220, f32[2048,4,128]{2,0,1:T(8,128)} %copy.47, f32[2048,128]{1,0:T(8,128)S(1)} %copy.50, f32[2048,128]{1,0:T(8,128)S(1)} %copy.46), kind=kLoop, calls=%fused_computation.42 | loop fusion | flops 5242880 | bytes 12582912 | tf_op jit(solution)/shard_map/convert_element_type | solution.py:193
  409.8 58.4 %while.13 = (s32[]{:T(128)}, bf16[2048,512]{1,0:T(8,128)(2,1)S(1)}, s32[]{:T(128)}, bf16[2560,128]{0,1:T(8,128)(2,1)}, s32[2048]{0:T(1024)S(1)}, /*index=5*/s32[...) while((s32[]{:T(128)}, bf16[2048,512]{1,0:T(8,128)(2,1)S(1)}, ...), condition=%wide.region_10.11_spmd, body=%wide.region_7.10_spmd.sunk | while | flops 1088949760 | bytes 21550328 | solution.py:90
  410.1 0.7 broadcast_compare_fusion.6
  410.9 0.7 broadcast_compare_fusion.5
  411.6 0.9 and_and_fusion.2
  412.6 7.5 %fusion.81 = (f32[4,512]{1,0:T(4,128)S(1)}, f32[4,512,1024]{1,2,0:T(8,128)}) fusion(pred[512,1024]{0,1:T(8,128)(4,1)S(1)} %and_and_fusion.2, bf16[2048,4,128]{2,0,1:T(8,128)(2,1)} %get-tuple-element.330, s32[]{:T(128)S(6)} %select_n.269, bf16[2560,128]{0,1:T(8,128)(2,1)} %get-tuple-element.329, s32[]{:T(128)S(6)} %select_n.270), kind=kOutput, calls=%fused_computation.112.clone.1 | convolution fusion | flops 545260544 | bytes 9707528 | tf_op jit(solution)/shard_map/while/body/eval_jaxpr/sub | solution.py:81
  420.1 4.2 fusion.82
  424.6 0.7 broadcast_compare_fusion.6
  425.4 0.7 broadcast_compare_fusion.5
  426.2 0.9 and_and_fusion.2
  427.1 7.6 %fusion.81 = (f32[4,512]{1,0:T(4,128)S(1)}, f32[4,512,1024]{1,2,0:T(8,128)}) fusion(pred[512,1024]{0,1:T(8,128)(4,1)S(1)} %and_and_fusion.2, bf16[2048,4,128]{2,0,1:T(8,128)(2,1)} %get-tuple-element.330, s32[]{:T(128)S(6)} %select_n.269, bf16[2560,128]{0,1:T(8,128)(2,1)} %get-tuple-element.329, s32[]{:T(128)S(6)} %select_n.270), kind=kOutput, calls=%fused_computation.112.clone.1 | convolution fusion | flops 545260544 | bytes 9707528 | tf_op jit(solution)/shard_map/while/body/eval_jaxpr/sub | solution.py:81
  434.6 4.2 fusion.82
  439.2 0.7 broadcast_compare_fusion.6
  440.0 0.7 broadcast_compare_fusion.5
  440.7 0.9 and_and_fusion.2
  441.6 7.5 %fusion.81 = (f32[4,512]{1,0:T(4,128)S(1)}, f32[4,512,1024]{1,2,0:T(8,128)}) fusion(pred[512,1024]{0,1:T(8,128)(4,1)S(1)} %and_and_fusion.2, bf16[2048,4,128]{2,0,1:T(8,128)(2,1)} %get-tuple-element.330, s32[]{:T(128)S(6)} %select_n.269, bf16[2560,128]{0,1:T(8,128)(2,1)} %get-tuple-element.329, s32[]{:T(128)S(6)} %select_n.270), kind=kOutput, calls=%fused_computation.112.clone.1 | convolution fusion | flops 545260544 | bytes 9707528 | tf_op jit(solution)/shard_map/while/body/eval_jaxpr/sub | solution.py:81
  449.2 4.2 fusion.82
  453.7 0.7 broadcast_compare_fusion.6
  454.5 0.7 broadcast_compare_fusion.5
  455.3 0.9 and_and_fusion.2
  456.2 7.5 %fusion.81 = (f32[4,512]{1,0:T(4,128)S(1)}, f32[4,512,1024]{1,2,0:T(8,128)}) fusion(pred[512,1024]{0,1:T(8,128)(4,1)S(1)} %and_and_fusion.2, bf16[2048,4,128]{2,0,1:T(8,128)(2,1)} %get-tuple-element.330, s32[]{:T(128)S(6)} %select_n.269, bf16[2560,128]{0,1:T(8,128)(2,1)} %get-tuple-element.329, s32[]{:T(128)S(6)} %select_n.270), kind=kOutput, calls=%fused_computation.112.clone.1 | convolution fusion | flops 545260544 | bytes 9707528 | tf_op jit(solution)/shard_map/while/body/eval_jaxpr/sub | solution.py:81
  463.7 4.2 fusion.82
  468.2 1.3 copy-done.2
  469.5 1.2 copy-done.1
  (88 shorter events, 5.1 us)
Async XLA Ops:
  6.5 1.2 copy-start
  9.2 8.3 %copy-start.11 = (s32[32]{0:T(128)S(1)}, s32[32]{0:T(128)}, u32[]{:S(2)}) copy-start(s32[32]{0:T(128)} %param.17) | copy-start | bytes 388
  9.3 8.7 %copy-start.9 = (s32[32]{0:T(128)S(1)}, s32[32]{0:T(128)}, u32[]{:S(2)}) copy-start(s32[32]{0:T(128)} %param.18) | copy-start | bytes 388
  11.7 32.0 %all-to-all-start = ((bf16[8,16,8192]{2,1,0:T(8,128)(2,1)}), bf16[8,16,8192]{2,1,0:T(8,128)(2,1)S(1)}, u32[]{:S(2)}, u32[]{:S(2)}) async-start(bf16[8,16,8192]{2,1,0:T(8,128)(2,1)} %copy.45), calls=%async_computation | async-start | bytes 4194304 | tf_op jit(solution)/shard_map/all_to_all | solution.py:124
  47.0 69.6 %all-to-all-start.1 = ((bf16[16,16,8192]{2,1,0:T(8,128)(2,1)}), bf16[16,16,8192]{2,1,0:T(8,128)(2,1)}, u32[]{:S(2)}, u32[]{:S(2)}) async-start(bf16[16,16,8192]{2,1,0:T(8,128)(2,1)} %bitcast.73), calls=%async_computation.1 | async-start | bytes 8388608 | tf_op jit(solution)/shard_map/all_to_all | solution.py:144
  54.8 268.9 %all-gather.2.cloned.1.call-start = ((), (), s32[]{:S(2)}) async-start(), calls=%async_computation.2 | async-start | bytes 35651584 | tf_op jit(solution)/shard_map/all_gather | solution.py:169
  123.0 2.9 copy-start.8
  125.9 2.0 copy-start.7
  125.9 2.6 copy-start.12
  125.9 2.6 copy-start.13
  125.9 197.8 %copy-start.5 = (bf16[8192,64]{0,1:T(8,128)(2,1)S(1)}, bf16[8192,64]{0,1:T(8,128)(2,1)}, u32[]{:S(2)}) copy-start(bf16[8192,64]{0,1:T(8,128)(2,1)} %param.24) | copy-start | bytes 3145732
  131.7 208.1 %copy-start.6 = (bf16[8192,64]{0,1:T(8,128)(2,1)S(1)}, bf16[8192,64]{0,1:T(8,128)(2,1)}, u32[]{:S(2)}) copy-start(bf16[8192,64]{0,1:T(8,128)(2,1)} %param.23) | copy-start | bytes 3145732
  339.9 17.6 %copy-start.10 = (f32[512]{0:T(512)S(1)}, f32[512]{0:T(512)}, u32[]{:S(2)}) copy-start(f32[512]{0:T(512)} %param.25) | copy-start | bytes 6148
  356.2 39.5 %collective-permute-start = (f32[2048,128]{0,1:T(8,128)S(1)}, f32[2048,128]{0,1:T(8,128)S(1)}, u32[]{:S(2)}, u32[]{:S(2)}) collective-permute-start(f32[2048,128]{0,1:T(8,128)S(1)} %maximum_add_fusion), channel_id=1, source_target_pairs={{0,1},{1,0},{2,3},{3,2},{4,5},{5,4},{6,7},{7,6},{8,9},{9,8},{10,11... | collective-permute-start | bytes 3145736 | tf_op jit(solution)/shard_map/ppermute | solution.py:19
  395.8 1.1 copy-start.3
  395.8 1.2 copy-start.4
  468.2 1.3 copy-start.2
  469.5 1.2 copy-start.1
Sparse Core Ops, SparseCore 0:
  128.0 195.6 all-gather.1
where the time goes:
time: 478 us
  waiting for transfers between devices  279 us (58%)
  matrix products  109 us (23%)
  other arithmetic  36.5 us (8%)
  local copies, waits for them, and re-layouts  24.2 us (5%)
  starting transfers between devices  14.9 us (3%)
  between operations  13.7 us (3%)
    all_gather x1, waiting for transfers between devices, per_device(): row_block = lax.all_gather(normed, 'seq', axis=0, tiled=True)  192 us
    all_to_all x1, waiting for transfers between devices, per_device(): lax.all_to_all(forward.reshape(member_count, capacity, feature_count), 's...  61.4 us
    sub x4, matrix products, one_block(): exponent = jnp.exp(scores - row_peak)  30.2 us
    all_to_all x1, waiting for transfers between devices, per_device(): lax.all_to_all(outgoing, 'dp', split_axis=0, concat_axis=0, tiled=True)  25.3 us
    dot_general x1, matrix products, per_device(): jnp.dot(row_block, q_weight, preferred_element_type=jnp.float32)  25 us
    dot_general x4, matrix products, one_block(): jnp.einsum('hqk,kd->qhd', weights, value_part, preferred_element_type=jnp...  16.9 us
    dot_general x1, matrix products, per_device(): jnp.dot(row_block, k_weight, preferred_element_type=jnp.float32)  16.2 us
    dot_general x1, matrix products, per_device(): jnp.dot(row_block, v_weight, preferred_element_type=jnp.float32)  16.2 us
  transfers between devices with their start and end apart: 4, of which 3 were waited for; matrix products, arithmetic and copies ran while one was open for 9% of the time, Pallas kernels for 0%

commit v1 on v0

--- a/solution.py
+++ b/solution.py
@@ -166,7 +166,8 @@
     image_part = jnp.take(landed.reshape(member_count * capacity, feature_count), source, axis=0)
     merged = jnp.where(covered[:, None], image_part, text_rows)
     normed = rms_norm(merged, norm_gain)
-    row_block = lax.all_gather(normed, "seq", axis=0, tiled=True)
+    repeated = jnp.stack([normed] * lax.axis_size("seq"))
+    row_block = jnp.concatenate(lax.all_to_all(repeated, "seq", 0, 0), axis=0)
     projected = jnp.concatenate(
         [
             jnp.dot(row_block, q_weight, preferred_element_type=jnp.float32),

time: 478 us -> 781 us (1.63)
  waiting for transfers between devices: 279 us -> 578 us
  between operations: 13.7 us -> 0.35 us
  local copies, waits for them, and re-layouts: 24.2 us -> 35.1 us
    all_to_all x0 -> x1, waiting for transfers between devices: none -> 491 us  [per_device(): row_block = jnp.concatenate(lax.all_to_all(repeated, 'seq', 0, 0), axis=0)]
    all_gather x1 -> x0, waiting for transfers between devices: 192 us -> none  [per_device(): row_block = lax.all_gather(normed, 'seq', axis=0, tiled=True)]
    another operation x1 -> x2, local copies, waits for them, and re-layouts: 0.11 us -> 11.1 us  [the longest x1 11 us: per_device(): repeated = jnp.stack([normed] * lax.axis_size('seq'))]
  transfers between devices with their start and end apart: 4 -> 4, of which waited for: 3 -> 3; matrix products, arithmetic and copies ran while one was open for 9% -> 6% of each run, Pallas kernels for 0% -> 0%
where the time goes in v1:
time: 781 us; the launch traced here: 778 us
  waiting for transfers between devices  578 us (74%)
  matrix products  109 us (14%)
  local copies, waits for them, and re-layouts  35.1 us (4%)
  other arithmetic  34.9 us (4%)
  starting transfers between devices  20.2 us (3%)
    all_to_all x1, waiting for transfers between devices, per_device(): row_block = jnp.concatenate(lax.all_to_all(repeated, 'seq', 0, 0), axis=0)  491 us
    all_to_all x1, waiting for transfers between devices, per_device(): lax.all_to_all(forward.reshape(member_count, capacity, feature_count), 's...  61.5 us
    sub x4, matrix products, one_block(): exponent = jnp.exp(scores - row_peak)  30.2 us
    all_to_all x1, waiting for transfers between devices, per_device(): lax.all_to_all(outgoing, 'dp', split_axis=0, concat_axis=0, tiled=True)  25.3 us
    dot_general x1, matrix products, per_device(): jnp.dot(row_block, q_weight, preferred_element_type=jnp.float32)  25 us
    dot_general x4, matrix products, one_block(): jnp.einsum('hqk,kd->qhd', weights, value_part, preferred_element_type=jnp...  16.9 us
    dot_general x1, matrix products, per_device(): jnp.dot(row_block, k_weight, preferred_element_type=jnp.float32)  16.3 us
    dot_general x1, matrix products, per_device(): jnp.dot(row_block, v_weight, preferred_element_type=jnp.float32)  16.2 us
  transfers between devices with their start and end apart: 4, of which 3 were waited for; matrix products, arithmetic and copies ran while one was open for 6% of the time, Pallas kernels for 0%

profile of v1, /device:TPU:1, one launch (start us, length us, event | category | flops | bytes accessed | tf_op | source)
XLA Modules:
  0.0 778.4 jit_solution(7467490565654643099)
XLA Ops:
  0.0 0.8 dynamic_slice.45
  1.2 1.5 convolution_convert_fusion.1
  2.7 2.5 copy.45
  5.2 5.8 all-to-all-start
  11.9 25.3 %all-to-all-done = bf16[8,16,8192]{2,1,0:T(8,128)(2,1)S(1)} async-done(((bf16[8,16,8192]{2,1,0:T(8,128)(2,1)}), bf16[8,16,8192]{2,1,0:T(8,128)(2,1)S(1)}, u32[]{:S(2)}, u32[]{:S(2)}) %all-to-all-start) | async-done | bytes 2097184 | tf_op jit(solution)/shard_map/all_to_all | solution.py:124
  37.2 3.2 convolution_convert_fusion
  40.4 7.8 %all-to-all-start.1 = ((bf16[16,16,8192]{2,1,0:T(8,128)(2,1)}), bf16[16,16,8192]{2,1,0:T(8,128)(2,1)}, u32[]{:S(2)}, u32[]{:S(2)}) async-start(bf16[16,16,8192]{2,1,0:T(8,128)(2,1)} %bitcast.74), calls=%async_computation.1 | async-start | bytes 8388608 | tf_op jit(solution)/shard_map/all_to_all | solution.py:144
  48.5 61.5 %all-to-all-done.1 = bf16[16,16,8192]{2,1,0:T(8,128)(2,1)} async-done(((bf16[16,16,8192]{2,1,0:T(8,128)(2,1)}), bf16[16,16,8192]{2,1,0:T(8,128)(2,1)}, u32[]{:S(2)}, u32[]{:S(2)}) %all-to-all-start.1) | async-done | bytes 4194336 | tf_op jit(solution)/shard_map/all_to_all | solution.py:144
  110.0 6.5 gather_fusion
  116.5 2.8 fusion.34
  119.4 0.6 fusion.36
  119.9 11.0 %stack.2 = bf16[16,128,8192]{2,1,0:T(8,128)(2,1)} broadcast(bf16[128,8192]{1,0:T(8,128)(2,1)S(1)} %fusion.36), dimensions={1,2} | broadcast | bytes 35651584 | tf_op jit(solution)/shard_map/stack | solution.py:169
  130.9 6.3 all-to-all-start.2
  138.1 2.8 multiply_cosine_fusion
  140.9 491.3 %all-to-all-done.2 = bf16[16,128,8192]{2,1,0:T(8,128)(2,1)} async-done(((bf16[16,128,8192]{2,1,0:T(8,128)(2,1)}), bf16[16,128,8192]{2,1,0:T(8,128)(2,1)}, u32[]{:S(2)}, u32[]{:S(2)}) %all-to-all-start.2) | async-done | bytes 33554464 | tf_op jit(solution)/shard_map/all_to_all | solution.py:170
  632.2 16.3 %fusion.64 = f32[2048,64]{0,1:T(8,128)S(1)} fusion(bf16[2048,8192]{1,0:T(8,128)(2,1)} %bitcast.13, bf16[8192,64]{0,1:T(8,128)(2,1)S(1)} %copy-done.5), kind=kOutput, calls=%fused_computation.113 | convolution fusion | flops 2147483648 | bytes 35127296 | tf_op jit(solution)/shard_map/dot_general | solution.py:174
  648.5 16.2 %fusion.65 = f32[2048,64]{0,1:T(8,128)S(1)} fusion(bf16[2048,8192]{1,0:T(8,128)(2,1)} %bitcast.13, bf16[8192,64]{0,1:T(8,128)(2,1)S(1)} %copy-done.6), kind=kOutput, calls=%fused_computation.114 | convolution fusion | flops 2147483648 | bytes 35127296 | tf_op jit(solution)/shard_map/dot_general | solution.py:175
  665.1 25.0 %convolution_add_fusion = f32[2048,512]{0,1:T(8,128)} fusion(bf16[2048,8192]{1,0:T(8,128)(2,1)} %bitcast.13, bf16[8192,512]{1,0:T(8,128)(2,1)} %param.22, f32[512]{0:T(512)S(1)} %copy-done.10), kind=kOutput, calls=%fused_computation.43 | convolution fusion | flops 17180917760 | bytes 46139392 | tf_op jit(solution)/shard_map/dot_general | solution.py:173
  690.1 5.3 copy.47
  695.4 7.9 %slice_negate_fusion = (f32[2048,4,64]{2,0,1:T(8,128)}, f32[2048,4,64]{2,0,1:T(8,128)}) fusion(f32[2048,4,128]{2,0,1:T(8,128)} %copy.47), kind=kLoop, calls=%fused_computation.39 | loop fusion | flops 524288 | bytes 8388608 | tf_op jit(solution)/shard_map/neg | solution.py:45
  703.8 0.7 slice.63
  704.6 1.1 pad_maximum_fusion
  706.3 2.0 concatenate.52
  708.3 1.9 fusion.44
  710.2 7.1 fusion.38
  717.4 58.4 %while.13 = (s32[]{:T(128)}, bf16[2048,512]{1,0:T(8,128)(2,1)S(1)}, s32[]{:T(128)}, bf16[2560,128]{0,1:T(8,128)(2,1)}, s32[2048]{0:T(1024)S(1)}, /*index=5*/s32[...) while((s32[]{:T(128)}, bf16[2048,512]{1,0:T(8,128)(2,1)S(1)}, ...), condition=%wide.region_10.11_spmd, body=%wide.region_7.10_spmd.sunk | while | flops 1088949760 | bytes 21550328 | solution.py:90
  717.7 0.7 broadcast_compare_fusion.5
  718.6 0.9 and_and_fusion.2
  719.5 7.6 fusion.81
  727.1 0.7 broadcast_compare_fusion.6
  727.7 4.2 fusion.82
  732.2 0.7 broadcast_compare_fusion.5
  733.1 0.9 and_and_fusion.2
  734.1 7.5 fusion.81
  741.6 0.7 broadcast_compare_fusion.6
  742.2 4.2 fusion.82
  746.8 0.7 broadcast_compare_fusion.5
  747.7 0.9 and_and_fusion.2
  748.6 7.6 fusion.81
  756.1 0.7 broadcast_compare_fusion.6
  756.8 4.2 fusion.82
  761.3 0.7 broadcast_compare_fusion.5
  762.2 0.9 and_and_fusion.2
  763.1 7.5 fusion.81
  770.7 0.7 broadcast_compare_fusion.6
  771.3 4.2 fusion.82
  775.8 1.3 copy-done.2
  777.1 1.2 copy-done.1
  (88 shorter events, 5.7 us)
Async XLA Ops:
  0.0 1.2 copy-start
  2.7 8.3 %copy-start.11 = (s32[32]{0:T(128)S(1)}, s32[32]{0:T(128)}, u32[]{:S(2)}) copy-start(s32[32]{0:T(128)} %param.17) | copy-start | bytes 388
  2.7 8.4 %copy-start.9 = (s32[32]{0:T(128)S(1)}, s32[32]{0:T(128)}, u32[]{:S(2)}) copy-start(s32[32]{0:T(128)} %param.18) | copy-start | bytes 388
  5.2 32.0 %all-to-all-start = ((bf16[8,16,8192]{2,1,0:T(8,128)(2,1)}), bf16[8,16,8192]{2,1,0:T(8,128)(2,1)S(1)}, u32[]{:S(2)}, u32[]{:S(2)}) async-start(bf16[8,16,8192]{2,1,0:T(8,128)(2,1)} %copy.45), calls=%async_computation | async-start | bytes 4194304 | tf_op jit(solution)/shard_map/all_to_all | solution.py:124
  40.4 69.6 %all-to-all-start.1 = ((bf16[16,16,8192]{2,1,0:T(8,128)(2,1)}), bf16[16,16,8192]{2,1,0:T(8,128)(2,1)}, u32[]{:S(2)}, u32[]{:S(2)}) async-start(bf16[16,16,8192]{2,1,0:T(8,128)(2,1)} %bitcast.74), calls=%async_computation.1 | async-start | bytes 8388608 | tf_op jit(solution)/shard_map/all_to_all | solution.py:144
  116.5 2.8 copy-start.8
  130.9 6.3 copy-start.7
  130.9 6.9 copy-start.12
  130.9 6.9 copy-start.13
  130.9 501.3 %copy-start.5 = (bf16[8192,64]{0,1:T(8,128)(2,1)S(1)}, bf16[8192,64]{0,1:T(8,128)(2,1)}, u32[]{:S(2)}) copy-start(bf16[8192,64]{0,1:T(8,128)(2,1)} %param.23) | copy-start | bytes 3145732
  130.9 501.3 %all-to-all-start.2 = ((bf16[16,128,8192]{2,1,0:T(8,128)(2,1)}), bf16[16,128,8192]{2,1,0:T(8,128)(2,1)}, u32[]{:S(2)}, u32[]{:S(2)}) async-start(bf16[16,128,8192]{2,1,0:T(8,128)(2,1)} %stack.2), calls=%async_computation.2 | async-start | bytes 67108864 | tf_op jit(solution)/shard_map/all_to_all | solution.py:170
  632.2 16.3 %copy-start.6 = (bf16[8192,64]{0,1:T(8,128)(2,1)S(1)}, bf16[8192,64]{0,1:T(8,128)(2,1)}, u32[]{:S(2)}) copy-start(bf16[8192,64]{0,1:T(8,128)(2,1)} %param.24) | copy-start | bytes 3145732
  648.5 16.7 %copy-start.10 = (f32[512]{0:T(512)S(1)}, f32[512]{0:T(512)}, u32[]{:S(2)}) copy-start(f32[512]{0:T(512)} %param.25) | copy-start | bytes 6148
  664.8 38.6 %collective-permute-start = (f32[2048,128]{0,1:T(8,128)S(1)}, f32[2048,128]{0,1:T(8,128)S(1)}, u32[]{:S(2)}, u32[]{:S(2)}) collective-permute-start(f32[2048,128]{0,1:T(8,128)S(1)} %maximum_add_fusion), channel_id=1, source_target_pairs={{0,1},{1,0},{2,3},{3,2},{4,5},{5,4},{6,7},{7,6},{8,9},{9,8},{10,11... | collective-permute-start | bytes 3145736 | tf_op jit(solution)/shard_map/ppermute | solution.py:19
  703.4 1.1 copy-start.3
  703.4 1.2 copy-start.4
  775.8 1.3 copy-start.2
  777.1 1.2 copy-start.1
